TPU v7x, 32 devices: a whole 2x2x4 slice. The times are simulated.
32 devices in a mesh: tm: 8 (over z, y), node: 4 (over x, core).
Axes of the slice: x: 2, y: 2, z: 4, core: 2. Of those that a mesh axis runs over, the one named last changes fastest.
Arguments:
- slice_starts: float32 [8, 32, 16384], P('tm'), may hold values from -1 to 1
- coupling: float32 [32, 16384], replicated, may hold values from 0.03 to 0.25
Outputs:
- node_values: float32 [8, 4, 32, 16384], P('tm', 'node')
- residual_log: float32 [3, 32], replicated
All inputs are finite; a program needn't handle non-finite values.
Results may differ from a plain program's by a relative error of at most 0.0001.
Values sent between devices are 32-bit elements.
A program may use at most 128 MiB of HBM per device.

v0:
```python
import jax
import jax.numpy as jnp
from jax import lax
from jax.sharding import PartitionSpec as P

M = 4
SWEEPS = 3
NEWTON = 2
time_step = 0.5
log_floor = 0.05


def spread(value, axis, root):
    mine = lax.axis_index(axis) == root
    return lax.psum(jnp.where(mine, value, jnp.zeros_like(value)), axis)


def passed_along(value, axis, by):
    size = lax.axis_size(axis)
    pairs = [(i, i + by) for i in range(size) if 0 <= i + by < size]
    return lax.ppermute(value, axis, pairs)


def legendre_gap(point, node_count):
    before = 1.0
    current = point
    for degree in range(1, node_count):
        following = ((2 * degree + 1) * point * current - degree * before) / (degree + 1)
        before = current
        current = following
    return current - before


def collocation(node_count):
    points = []
    samples = 4000
    for sample_index in range(samples - 1):
        lower_end = -1.0 + 2.0 * sample_index / samples
        upper_end = -1.0 + 2.0 * (sample_index + 1) / samples
        lower_value = legendre_gap(lower_end, node_count)
        upper_value = legendre_gap(upper_end, node_count)
        if lower_value * upper_value < 0.0:
            for halving in range(80):
                middle = 0.5 * (lower_end + upper_end)
                middle_value = legendre_gap(middle, node_count)
                if lower_value * middle_value <= 0.0:
                    upper_end = middle
                else:
                    lower_end = middle
                    lower_value = middle_value
            points.append(0.5 * (lower_end + upper_end))
    points.append(1.0)
    node_times = [(point + 1.0) / 2.0 for point in points]
    matrix = [[0.0] * node_count for row_index in range(node_count)]
    for column in range(node_count):
        coeffs = [1.0]
        for other in range(node_count):
            if other != column:
                scale = node_times[column] - node_times[other]
                shifted = [0.0] + coeffs
                scaled = [value * node_times[other] for value in coeffs] + [0.0]
                coeffs = [(shifted[power] - scaled[power]) / scale for power in range(len(shifted))]
        for row_index in range(node_count):
            upper_time = node_times[row_index]
            matrix[row_index][column] = sum(
                (
                    coeffs[power] * upper_time ** (power + 1) / (power + 1)
                    for power in range(len(coeffs))
                )
            )
    return (node_times, matrix)


def operator_term(field_values, coupling):
    right_side = jnp.roll(field_values, -1, axis=-1)
    left_side = jnp.roll(field_values, 1, axis=-1)
    left_coupling = jnp.roll(coupling, 1, axis=-1)
    cubic = field_values * field_values * field_values
    return (
        coupling * (right_side - field_values)
        - left_coupling * (field_values - left_side)
        + field_values
        - cubic
    )


def body(slice_starts, coupling):
    node_times, matrix = collocation(M)
    weights = jnp.asarray(matrix, jnp.float32)
    diag_weights = jnp.asarray([time_step * moment / M for moment in node_times], jnp.float32)
    node_pos = lax.axis_index("node")
    slice_pos = lax.axis_index("tm")
    systems, cells = coupling.shape
    initial = slice_starts[0]
    implicit = diag_weights[node_pos]
    row_weights = weights[node_pos]
    node_state = initial
    totals = []
    for sweep_index in range(SWEEPS):
        if sweep_index == 0:
            end_value = initial
        else:
            end_value = spread(node_state, "node", M - 1)
        arrived = passed_along(end_value, "tm", 1)
        start_value = jnp.where(slice_pos == 0, initial, arrived)
        forcing = operator_term(node_state, coupling)
        segment = lax.all_gather(forcing, "node", axis=0, tiled=True)
        positions = jnp.arange(segment.shape[0], dtype=jnp.int32)
        owners = positions // systems
        members = positions % systems
        factors = jnp.sum(
            jnp.where(
                owners[:, None] == jnp.arange(M, dtype=jnp.int32)[None], row_weights[None], 0.0
            ),
            axis=1,
        )
        select = jnp.where(
            jnp.arange(systems, dtype=jnp.int32)[:, None] == members[None], factors[None], 0.0
        )
        quadrature = jnp.zeros_like(forcing) + jnp.dot(
            select, segment, precision=lax.Precision.HIGHEST
        )
        base = start_value + time_step * quadrature
        defect = base - node_state
        partial_value = jnp.sum(defect * defect, axis=1)
        totals.append(lax.psum(partial_value, ("tm", "node")))
        target = base - implicit * (node_state - node_state * node_state * node_state)
        iterate = node_state
        for newton_step in range(NEWTON):
            cubic = iterate * iterate * iterate
            derivative = 1.0 - implicit + 3.0 * implicit * iterate * iterate
            iterate = iterate - (iterate - implicit * (iterate - cubic) - target) / derivative
        node_state = iterate
    summed = jnp.stack(totals)
    cell_total = lax.axis_size("tm") * M * cells
    residual_log = jnp.log(log_floor + summed / cell_total)
    return (node_state[None, None], residual_log)


def solution(mesh):
    placed = (P("tm", None, None), P())
    return jax.shard_map(
        body,
        mesh=mesh,
        in_specs=placed,
        out_specs=(P("tm", "node", None, None), P()),
        check_vma=False,
    )
```

profile of v0, /device:TPU:0, one launch (start us, length us, event | category | flops | bytes accessed | tf_op | source)
XLA Modules:
  0.0 382.4 jit_solution(9539708886038330631)
XLA Ops:
  7.2 0.0 all-gather.4.cloned.1.call-start
  7.2 0.8 fusion.81
  8.0 0.0 copy-start
  8.0 0.0 copy-start.1
  8.0 3.0 fusion.82
  11.1 0.0 copy-done
  11.1 0.1 slice.52
  11.2 0.4 copy-done.1
  11.5 2.5 fusion
  14.0 0.0 copy-start.5
  14.0 0.0 all-gather.4.cloned.1.call-update
  14.0 0.0 all-reduce.4.cloned.1.call-start
  14.1 6.3 %collective-permute-start = (f32[32,16384]{1,0:T(8,128)}, f32[32,16384]{1,0:T(8,128)}, u32[]{:S(2)}, u32[]{:S(2)}) collective-permute-start(f32[32,16384]{1,0:T(8,128)} %bitcast.26), channel_id=1, source_target_pairs={{0,4},{4,8},{8,12},{12,16},{16,20},{20,24},{24,28},{1,5},{5,9},{9,... | collective-permute-start | bytes 6291464 | tf_op jit(solution)/shard_map/ppermute | solution.py:21
  20.3 0.0 copy-done.5
  20.3 0.6 dynamic_slice.6
  22.2 0.7 dynamic-slice_bitcast_fusion
  22.9 0.1 select_reduce_fusion
  23.0 41.1 %collective-permute-done = f32[32,16384]{1,0:T(8,128)} collective-permute-done((f32[32,16384]{1,0:T(8,128)}, f32[32,16384]{1,0:T(8,128)}, u32[]{:S(2)}, u32[]{:S(2)}) %collective-permute-start) | collective-permute-done | bytes 2097184 | tf_op jit(solution)/shard_map/ppermute | solution.py:21
  64.2 11.0 %all-gather.4.cloned.1.call-done = f32[128,16384]{1,0:T(8,128)} async-done(((f32[32,16384]{1,0:T(8,128)}), f32[128,16384]{1,0:T(8,128)}) %all-gather.4.cloned.1.call-update) | async-done | bytes 8388624 | tf_op jit(solution)/shard_map/all_gather | solution.py:107
  75.2 10.5 %broadcast_select_fusion.1 = (f32[32,16384]{1,0:T(8,128)}, f32[32,16384]{1,0:T(8,128)S(1)}, f32[32]{0:T(128)S(1)}) fusion(pred[]{:T(512)S(6)} %eq.27, f32[]{:T(128)S(6)} %mul.175, f32[]{:T(128)S(6)} %sub.156, f32[32,16384]{1,0:T(8,128)} %collective-permute-done, pred[]{:T(512)S(6)} %eq.20, f32[]{:T(128)} %bitcast.1, f32[1,32,16384]{2,1,0:T(8,128)} %param.4, ...), kind=kOutput, calls=%fused_computation.87 | convolution fusion | flops 821043200 | bytes 16778382 | tf_op jit(solution)/shard_map/dot_general | solution.py:120
  85.6 0.0 copy-start.4
  85.6 0.1 fusion.79
  85.7 2.6 fusion.80
  88.3 0.0 copy-done.4
  88.3 0.0 all-reduce.4.cloned.1.call-update
  88.4 0.0 all-gather.6.cloned.1.call-start
  88.4 5.3 %fusion.2 = f32[32,16384]{1,0:T(8,128)} fusion(f32[32,16384]{1,0:T(8,128)} %copy-done.4, f32[32,16384]{1,0:T(8,128)S(1)} %copy-done, f32[32,1]{1,0:T(8,128)S(1)} %get-tuple-element.18, f32[32,16383]{1,0:T(8,128)} %get-tuple-element.20, f32[32,16383]{1,0:T(8,128)} %get-tuple-element.19, f32[32,1]{1,0:T(8,128)S(1)} %get-tuple-element.17, ...), kind=kLoop, calls=%fused_computation.17 | loop fusion | flops 6291456 | bytes 12582912 | tf_op jit(solution)/shard_map/sub | solution.py:80
  93.8 0.0 all-gather.6.cloned.1.call-update
  93.8 0.0 all-reduce.6.cloned.1.call-start
  93.8 46.4 %all-reduce.4.cloned.1.call-done = f32[32,16384]{1,0:T(8,128)} async-done(((f32[32,16384]{1,0:T(8,128)}), f32[32,16384]{1,0:T(8,128)}) %all-reduce.4.cloned.1.call-update) | async-done | bytes 2097168 | tf_op jit(solution)/shard_map/psum | solution.py:15
  140.2 4.7 %collective-permute-start.1 = (f32[32,16384]{1,0:T(8,128)}, f32[32,16384]{1,0:T(8,128)}, u32[]{:S(2)}, u32[]{:S(2)}) collective-permute-start(f32[32,16384]{1,0:T(8,128)} %all-reduce.4.cloned.1.call-done), channel_id=1, source_target_pairs={{0,4},{4,8},{8,12},{12,16},{16,20},{20,24},{24,28},{1,5},{5,9},{9,... | collective-permute-start | bytes 6291464 | tf_op jit(solution)/shard_map/ppermute | solution.py:21
  144.9 43.6 %collective-permute-done.1 = f32[32,16384]{1,0:T(8,128)} collective-permute-done((f32[32,16384]{1,0:T(8,128)}, f32[32,16384]{1,0:T(8,128)}, u32[]{:S(2)}, u32[]{:S(2)}) %collective-permute-start.1) | collective-permute-done | bytes 2097184 | tf_op jit(solution)/shard_map/ppermute | solution.py:21
  188.5 11.6 %all-gather.6.cloned.1.call-done = f32[128,16384]{1,0:T(8,128)} async-done(((f32[32,16384]{1,0:T(8,128)}), f32[128,16384]{1,0:T(8,128)}) %all-gather.6.cloned.1.call-update) | async-done | bytes 8388624 | tf_op jit(solution)/shard_map/all_gather | solution.py:107
  200.1 10.8 %broadcast_select_fusion = (f32[32,16384]{1,0:T(8,128)}, f32[32,16384]{1,0:T(8,128)S(1)}, f32[32]{0:T(128)S(1)}) fusion(pred[]{:T(512)S(6)} %eq.27, f32[32,16384]{1,0:T(8,128)} %copy-done.4, f32[]{:T(128)S(6)} %mul.175, f32[]{:T(128)S(6)} %sub.156, f32[]{:T(128)} %bitcast.1, f32[128,16384]{1,0:T(8,128)} %all-gather.6.cloned.1.call-done, ...), kind=kOutput, calls=%fused_computation.86 | convolution fusion | flops 821043200 | bytes 18875534 | tf_op jit(solution)/shard_map/dot_general | solution.py:120
  210.9 0.0 copy-start.3
  210.9 0.1 fusion.77
  211.0 2.6 fusion.78
  213.6 0.0 copy-done.3
  213.6 0.0 all-reduce.6.cloned.1.call-update
  213.7 0.2 all-gather.8.cloned.1.call-start
  213.9 5.3 %fusion.4 = f32[32,16384]{1,0:T(8,128)} fusion(f32[32,16384]{1,0:T(8,128)} %copy-done.3, f32[32,16384]{1,0:T(8,128)S(1)} %copy-done, f32[32,1]{1,0:T(8,128)S(1)} %get-tuple-element.14, f32[32,16383]{1,0:T(8,128)} %get-tuple-element.16, f32[32,16383]{1,0:T(8,128)} %get-tuple-element.15, f32[32,1]{1,0:T(8,128)S(1)} %get-tuple-element.13, ...), kind=kLoop, calls=%fused_computation.19 | loop fusion | flops 6291456 | bytes 12582912 | tf_op jit(solution)/shard_map/sub | solution.py:80
  219.2 0.0 copy-start.2
  219.2 0.0 all-gather.8.cloned.1.call-update
  219.3 46.2 %all-reduce.6.cloned.1.call-done = f32[32,16384]{1,0:T(8,128)} async-done(((f32[32,16384]{1,0:T(8,128)}), f32[32,16384]{1,0:T(8,128)}) %all-reduce.6.cloned.1.call-update) | async-done | bytes 2097168 | tf_op jit(solution)/shard_map/psum | solution.py:15
  265.5 4.7 %collective-permute-start.2 = (f32[32,16384]{1,0:T(8,128)}, f32[32,16384]{1,0:T(8,128)}, u32[]{:S(2)}, u32[]{:S(2)}) collective-permute-start(f32[32,16384]{1,0:T(8,128)} %all-reduce.6.cloned.1.call-done), channel_id=1, source_target_pairs={{0,4},{4,8},{8,12},{12,16},{16,20},{20,24},{24,28},{1,5},{5,9},{9,... | collective-permute-start | bytes 6291464 | tf_op jit(solution)/shard_map/ppermute | solution.py:21
  270.2 43.6 %collective-permute-done.2 = f32[32,16384]{1,0:T(8,128)} collective-permute-done((f32[32,16384]{1,0:T(8,128)}, f32[32,16384]{1,0:T(8,128)}, u32[]{:S(2)}, u32[]{:S(2)}) %collective-permute-start.2) | collective-permute-done | bytes 2097184 | tf_op jit(solution)/shard_map/ppermute | solution.py:21
  313.8 11.5 %all-gather.8.cloned.1.call-done = f32[128,16384]{1,0:T(8,128)} async-done(((f32[32,16384]{1,0:T(8,128)}), f32[128,16384]{1,0:T(8,128)}) %all-gather.8.cloned.1.call-update) | async-done | bytes 8388624 | tf_op jit(solution)/shard_map/all_gather | solution.py:107
  325.3 0.0 copy-done.2
  325.3 10.4 %multiply_reduce_fusion = (f32[32]{0:T(128)S(1)}, f32[1,1,32,16384]{3,2,1,0:T(8,128)}) fusion(f32[32,16384]{1,0:T(8,128)} %copy-done.3, f32[]{:T(128)S(6)} %mul.175, f32[]{:T(128)S(6)} %sub.156, f32[]{:T(128)} %bitcast.1, f32[128,16384]{1,0:T(8,128)} %all-gather.8.cloned.1.call-done, f32[128]{0:T(128)S(1)} %select_reduce_fusion, ...), kind=kOutput, calls=%fused_computation.79 | convolution fusion | flops 820518912 | bytes 16778380 | tf_op jit(solution)/shard_map/dot_general | solution.py:120
  335.7 39.6 %all-reduce = (f32[1,32]{1,0:T(1,128)S(1)}, f32[1,32]{1,0:T(1,128)S(1)}, f32[1,32]{1,0:T(1,128)S(1)}) all-reduce(f32[1,32]{1,0:T(1,128)S(1)} %bitcast.29, f32[1,32]{1,0:T(1,128)S(1)} %bitcast.28, f32[1,32]{1,0:T(1,128)S(1)} %bitcast.27), channel_id=1, replica_groups=mesh['tm'=8,'node'=4] {'tm','node'}, use_global_device_ids=true, to_apply=%region_8.9 | all-reduce | flops 96 | bytes 768 | tf_op jit(solution)/shard_map/psum | solution.py:126
  375.3 0.6 fusion.71
  (2 shorter events, 0.0 us)
Async XLA Ops:
  7.2 68.0 %all-gather.4.cloned.1.call-start = ((), (), s32[]{:S(2)}) async-start(), calls=%async_computation | async-start | bytes 10485760 | tf_op jit(solution)/shard_map/all_gather | solution.py:107
  8.0 3.1 copy-start
  8.0 3.5 copy-start.1
  14.0 6.4 %copy-start.5 = (f32[4]{0:T(128)S(1)}, f32[4]{0:T(128)}, u32[]{:S(2)}) copy-start(f32[4]{0:T(128)} %constant.74.clone) | copy-start | bytes 52
  14.0 126.2 %all-reduce.4.cloned.1.call-start = ((), (), s32[]{:S(2)}) async-start(), calls=%async_computation.1 | async-start | bytes 4194304 | tf_op jit(solution)/shard_map/psum | solution.py:15
  14.1 50.1 %collective-permute-start = (f32[32,16384]{1,0:T(8,128)}, f32[32,16384]{1,0:T(8,128)}, u32[]{:S(2)}, u32[]{:S(2)}) collective-permute-start(f32[32,16384]{1,0:T(8,128)} %bitcast.26), channel_id=1, source_target_pairs={{0,4},{4,8},{8,12},{12,16},{16,20},{20,24},{24,28},{1,5},{5,9},{9,... | collective-permute-start | bytes 6291464 | tf_op jit(solution)/shard_map/ppermute | solution.py:21
  85.6 2.7 copy-start.4
  88.4 111.8 %all-gather.6.cloned.1.call-start = ((), (), s32[]{:S(2)}) async-start(), calls=%async_computation.2 | async-start | bytes 10485760 | tf_op jit(solution)/shard_map/all_gather | solution.py:107
  93.8 171.7 %all-reduce.6.cloned.1.call-start = ((), (), s32[]{:S(2)}) async-start(), calls=%async_computation.3 | async-start | bytes 4194304 | tf_op jit(solution)/shard_map/psum | solution.py:15
  140.2 48.3 %collective-permute-start.1 = (f32[32,16384]{1,0:T(8,128)}, f32[32,16384]{1,0:T(8,128)}, u32[]{:S(2)}, u32[]{:S(2)}) collective-permute-start(f32[32,16384]{1,0:T(8,128)} %all-reduce.4.cloned.1.call-done), channel_id=1, source_target_pairs={{0,4},{4,8},{8,12},{12,16},{16,20},{20,24},{24,28},{1,5},{5,9},{9,... | collective-permute-start | bytes 6291464 | tf_op jit(solution)/shard_map/ppermute | solution.py:21
  210.9 2.7 copy-start.3
  213.7 111.6 %all-gather.8.cloned.1.call-start = ((), (), s32[]{:S(2)}) async-start(), calls=%async_computation.4 | async-start | bytes 10485760 | tf_op jit(solution)/shard_map/all_gather | solution.py:107
  219.2 106.0 %copy-start.2 = (f32[1,32,16384]{2,1,0:T(8,128)S(1)}, f32[1,32,16384]{2,1,0:T(8,128)}, u32[]{:S(2)}) copy-start(f32[1,32,16384]{2,1,0:T(8,128)} %param.4) | copy-start | bytes 6291460
  265.5 48.3 %collective-permute-start.2 = (f32[32,16384]{1,0:T(8,128)}, f32[32,16384]{1,0:T(8,128)}, u32[]{:S(2)}, u32[]{:S(2)}) collective-permute-start(f32[32,16384]{1,0:T(8,128)} %all-reduce.6.cloned.1.call-done), channel_id=1, source_target_pairs={{0,4},{4,8},{8,12},{12,16},{16,20},{20,24},{24,28},{1,5},{5,9},{9,... | collective-permute-start | bytes 6291464 | tf_op jit(solution)/shard_map/ppermute | solution.py:21
Sparse Core Ops, SparseCore 0:
  14.1 60.9 all-gather.3
  88.5 51.6 all-reduce.3
  141.8 58.3 all-gather.5
  213.8 51.6 all-reduce.5
  266.9 58.3 all-gather.7
where the time goes:
time: 383 us; the launch traced here: 382 us
  waiting for transfers between devices  255 us (67%)
  blocking collectives  39.6 us (10%)
  matrix products  31.7 us (8%)
  starting transfers between devices  16 us (4%)
  between operations  15.1 us (4%)
  other arithmetic  13.9 us (4%)
  local copies, waits for them, and re-layouts  10.9 us (3%)
    ppermute x3, waiting for transfers between devices, passed_along(): return lax.ppermute(value, axis, pairs)  128 us
    psum x2, waiting for transfers between devices, spread(): return lax.psum(jnp.where(mine, value, jnp.zeros_like(value)), axis)  92.6 us
    psum x1, blocking collectives, body(): totals.append(lax.psum(partial_value, ('tm', 'node')))  39.6 us
    all_gather x3, waiting for transfers between devices, body(): segment = lax.all_gather(forcing, 'node', axis=0, tiled=True)  34.1 us
    dot_general x3, matrix products, body(): jnp.dot(select, segment, precision=lax.Precision.HIGHEST)  31.7 us
    ppermute x3, starting transfers between devices, passed_along(): return lax.ppermute(value, axis, pairs)  15.6 us
    sub x3, other arithmetic, operator_term(): coupling * (right_side - field_values)  13.2 us
    slice x6, local copies, waits for them, and re-layouts, operator_term(): left_side = jnp.roll(field_values, 1, axis=-1)  9.22 us
  transfers between devices with their start and end apart: 8, of which 8 were waited for; matrix products, arithmetic and copies ran while one was open for 3% of the time, Pallas kernels for 0%

commit v1 on v0

--- a/solution.py
+++ b/solution.py
@@ -123,7 +123,7 @@
         base = start_value + time_step * quadrature
         defect = base - node_state
         partial_value = jnp.sum(defect * defect, axis=1)
-        totals.append(lax.psum(partial_value, ("tm", "node")))
+        totals.append(lax.psum(lax.psum(partial_value, "node"), "tm"))
         target = base - implicit * (node_state - node_state * node_state * node_state)
         iterate = node_state
         for newton_step in range(NEWTON):

time: 383 us -> 371 us (0.969)
  blocking collectives: 39.6 us -> 27.7 us
    psum x1 -> x2, blocking collectives: 39.6 us -> 27.7 us  [body(): totals.append(lax.psum(lax.psum(partial_value, 'node'), 'tm'))]
where the time goes in v1:
time: 371 us
  waiting for transfers between devices  255 us (69%)
  matrix products  31.7 us (9%)
  blocking collectives  27.7 us (7%)
  starting transfers between devices  16 us (4%)
  between operations  15.1 us (4%)
  other arithmetic  13.9 us (4%)
  local copies, waits for them, and re-layouts  11 us (3%)
    ppermute x3, waiting for transfers between devices, passed_along(): return lax.ppermute(value, axis, pairs)  128 us
    psum x2, waiting for transfers between devices, spread(): return lax.psum(jnp.where(mine, value, jnp.zeros_like(value)), axis)  92.6 us
    all_gather x3, waiting for transfers between devices, body(): segment = lax.all_gather(forcing, 'node', axis=0, tiled=True)  34.1 us
    dot_general x3, matrix products, body(): jnp.dot(select, segment, precision=lax.Precision.HIGHEST)  31.7 us
    psum x2, blocking collectives, body(): totals.append(lax.psum(lax.psum(partial_value, 'node'), 'tm'))  27.7 us
    ppermute x3, starting transfers between devices, passed_along(): return lax.ppermute(value, axis, pairs)  15.6 us
    sub x3, other arithmetic, operator_term(): coupling * (right_side - field_values)  13.2 us
    slice x6, local copies, waits for them, and re-layouts, operator_term(): left_side = jnp.roll(field_values, 1, axis=-1)  9.22 us
  transfers between devices with their start and end apart: 8, of which 8 were waited for; matrix products, arithmetic and copies ran while one was open for 3% of the time, Pallas kernels for 0%

profile of v1, /device:TPU:0, one launch (start us, length us, event | category | flops | bytes accessed | tf_op | source)
XLA Modules:
  0.0 370.5 jit_solution(1741457527429590860)
XLA Ops:
  7.2 0.0 all-gather.4.cloned.1.call-start
  7.2 0.8 fusion.81
  8.0 0.0 copy-start
  8.0 0.0 copy-start.1
  8.0 3.0 fusion.82
  11.1 0.0 copy-done
  11.1 0.1 slice.52
  11.2 0.4 copy-done.1
  11.5 2.5 fusion
  14.0 0.0 copy-start.5
  14.0 0.0 all-gather.4.cloned.1.call-update
  14.0 0.0 all-reduce.5.cloned.1.call-start
  14.1 6.3 %collective-permute-start = (f32[32,16384]{1,0:T(8,128)}, f32[32,16384]{1,0:T(8,128)}, u32[]{:S(2)}, u32[]{:S(2)}) collective-permute-start(f32[32,16384]{1,0:T(8,128)} %bitcast.26), channel_id=1, source_target_pairs={{0,4},{4,8},{8,12},{12,16},{16,20},{20,24},{24,28},{1,5},{5,9},{9,... | collective-permute-start | bytes 6291464 | tf_op jit(solution)/shard_map/ppermute | solution.py:21
  20.3 0.0 copy-done.5
  20.3 0.6 dynamic_slice.6
  22.3 0.7 dynamic-slice_bitcast_fusion
  23.0 0.1 select_reduce_fusion
  23.0 41.1 %collective-permute-done = f32[32,16384]{1,0:T(8,128)} collective-permute-done((f32[32,16384]{1,0:T(8,128)}, f32[32,16384]{1,0:T(8,128)}, u32[]{:S(2)}, u32[]{:S(2)}) %collective-permute-start) | collective-permute-done | bytes 2097184 | tf_op jit(solution)/shard_map/ppermute | solution.py:21
  64.2 11.0 %all-gather.4.cloned.1.call-done = f32[128,16384]{1,0:T(8,128)} async-done(((f32[32,16384]{1,0:T(8,128)}), f32[128,16384]{1,0:T(8,128)}) %all-gather.4.cloned.1.call-update) | async-done | bytes 8388624 | tf_op jit(solution)/shard_map/all_gather | solution.py:107
  75.2 10.5 %broadcast_select_fusion.1 = (f32[32,16384]{1,0:T(8,128)}, f32[32,16384]{1,0:T(8,128)S(1)}, f32[32]{0:T(128)S(1)}) fusion(pred[]{:T(512)S(6)} %eq.27, f32[]{:T(128)S(6)} %mul.175, f32[]{:T(128)S(6)} %sub.156, f32[32,16384]{1,0:T(8,128)} %collective-permute-done, pred[]{:T(512)S(6)} %eq.20, f32[]{:T(128)} %bitcast.1, f32[1,32,16384]{2,1,0:T(8,128)} %param.4, ...), kind=kOutput, calls=%fused_computation.87 | convolution fusion | flops 821043200 | bytes 16778382 | tf_op jit(solution)/shard_map/dot_general | solution.py:120
  85.6 0.0 copy-start.4
  85.6 0.1 fusion.79
  85.7 2.6 fusion.80
  88.3 0.0 copy-done.4
  88.3 0.0 all-reduce.5.cloned.1.call-update
  88.4 0.0 all-gather.6.cloned.1.call-start
  88.4 5.3 %fusion.2 = f32[32,16384]{1,0:T(8,128)} fusion(f32[32,16384]{1,0:T(8,128)} %copy-done.4, f32[32,16384]{1,0:T(8,128)S(1)} %copy-done, f32[32,1]{1,0:T(8,128)S(1)} %get-tuple-element.21, f32[32,16383]{1,0:T(8,128)} %get-tuple-element.23, f32[32,16383]{1,0:T(8,128)} %get-tuple-element.22, f32[32,1]{1,0:T(8,128)S(1)} %get-tuple-element.20, ...), kind=kLoop, calls=%fused_computation.17 | loop fusion | flops 6291456 | bytes 12582912 | tf_op jit(solution)/shard_map/sub | solution.py:80
  93.7 0.0 all-gather.6.cloned.1.call-update
  93.8 0.0 all-reduce.7.cloned.1.call-start
  93.8 46.4 %all-reduce.5.cloned.1.call-done = f32[32,16384]{1,0:T(8,128)} async-done(((f32[32,16384]{1,0:T(8,128)}), f32[32,16384]{1,0:T(8,128)}) %all-reduce.5.cloned.1.call-update) | async-done | bytes 2097168 | tf_op jit(solution)/shard_map/psum | solution.py:15
  140.2 4.7 %collective-permute-start.1 = (f32[32,16384]{1,0:T(8,128)}, f32[32,16384]{1,0:T(8,128)}, u32[]{:S(2)}, u32[]{:S(2)}) collective-permute-start(f32[32,16384]{1,0:T(8,128)} %all-reduce.5.cloned.1.call-done), channel_id=1, source_target_pairs={{0,4},{4,8},{8,12},{12,16},{16,20},{20,24},{24,28},{1,5},{5,9},{9,... | collective-permute-start | bytes 6291464 | tf_op jit(solution)/shard_map/ppermute | solution.py:21
  144.9 43.7 %collective-permute-done.1 = f32[32,16384]{1,0:T(8,128)} collective-permute-done((f32[32,16384]{1,0:T(8,128)}, f32[32,16384]{1,0:T(8,128)}, u32[]{:S(2)}, u32[]{:S(2)}) %collective-permute-start.1) | collective-permute-done | bytes 2097184 | tf_op jit(solution)/shard_map/ppermute | solution.py:21
  188.5 11.6 %all-gather.6.cloned.1.call-done = f32[128,16384]{1,0:T(8,128)} async-done(((f32[32,16384]{1,0:T(8,128)}), f32[128,16384]{1,0:T(8,128)}) %all-gather.6.cloned.1.call-update) | async-done | bytes 8388624 | tf_op jit(solution)/shard_map/all_gather | solution.py:107
  200.1 10.8 %broadcast_select_fusion = (f32[32,16384]{1,0:T(8,128)}, f32[32,16384]{1,0:T(8,128)S(1)}, f32[32]{0:T(128)S(1)}) fusion(pred[]{:T(512)S(6)} %eq.27, f32[32,16384]{1,0:T(8,128)} %copy-done.4, f32[]{:T(128)S(6)} %mul.175, f32[]{:T(128)S(6)} %sub.156, f32[]{:T(128)} %bitcast.1, f32[128,16384]{1,0:T(8,128)} %all-gather.6.cloned.1.call-done, ...), kind=kOutput, calls=%fused_computation.86 | convolution fusion | flops 821043200 | bytes 18875534 | tf_op jit(solution)/shard_map/dot_general | solution.py:120
  210.9 0.0 copy-start.3
  210.9 0.1 fusion.77
  211.0 2.6 fusion.78
  213.6 0.0 copy-done.3
  213.6 0.0 all-reduce.7.cloned.1.call-update
  213.7 0.2 all-gather.8.cloned.1.call-start
  213.9 5.3 %fusion.4 = f32[32,16384]{1,0:T(8,128)} fusion(f32[32,16384]{1,0:T(8,128)} %copy-done.3, f32[32,16384]{1,0:T(8,128)S(1)} %copy-done, f32[32,1]{1,0:T(8,128)S(1)} %get-tuple-element.17, f32[32,16383]{1,0:T(8,128)} %get-tuple-element.19, f32[32,16383]{1,0:T(8,128)} %get-tuple-element.18, f32[32,1]{1,0:T(8,128)S(1)} %get-tuple-element.16, ...), kind=kLoop, calls=%fused_computation.19 | loop fusion | flops 6291456 | bytes 12582912 | tf_op jit(solution)/shard_map/sub | solution.py:80
  219.2 0.0 copy-start.2
  219.2 0.0 all-gather.8.cloned.1.call-update
  219.3 46.2 %all-reduce.7.cloned.1.call-done = f32[32,16384]{1,0:T(8,128)} async-done(((f32[32,16384]{1,0:T(8,128)}), f32[32,16384]{1,0:T(8,128)}) %all-reduce.7.cloned.1.call-update) | async-done | bytes 2097168 | tf_op jit(solution)/shard_map/psum | solution.py:15
  265.5 4.7 %collective-permute-start.2 = (f32[32,16384]{1,0:T(8,128)}, f32[32,16384]{1,0:T(8,128)}, u32[]{:S(2)}, u32[]{:S(2)}) collective-permute-start(f32[32,16384]{1,0:T(8,128)} %all-reduce.7.cloned.1.call-done), channel_id=1, source_target_pairs={{0,4},{4,8},{8,12},{12,16},{16,20},{20,24},{24,28},{1,5},{5,9},{9,... | collective-permute-start | bytes 6291464 | tf_op jit(solution)/shard_map/ppermute | solution.py:21
  270.2 43.7 %collective-permute-done.2 = f32[32,16384]{1,0:T(8,128)} collective-permute-done((f32[32,16384]{1,0:T(8,128)}, f32[32,16384]{1,0:T(8,128)}, u32[]{:S(2)}, u32[]{:S(2)}) %collective-permute-start.2) | collective-permute-done | bytes 2097184 | tf_op jit(solution)/shard_map/ppermute | solution.py:21
  313.8 11.5 %all-gather.8.cloned.1.call-done = f32[128,16384]{1,0:T(8,128)} async-done(((f32[32,16384]{1,0:T(8,128)}), f32[128,16384]{1,0:T(8,128)}) %all-gather.8.cloned.1.call-update) | async-done | bytes 8388624 | tf_op jit(solution)/shard_map/all_gather | solution.py:107
  325.3 0.0 copy-done.2
  325.3 10.4 %multiply_reduce_fusion = (f32[32]{0:T(128)S(1)}, f32[1,1,32,16384]{3,2,1,0:T(8,128)}) fusion(f32[32,16384]{1,0:T(8,128)} %copy-done.3, f32[]{:T(128)S(6)} %mul.175, f32[]{:T(128)S(6)} %sub.156, f32[]{:T(128)} %bitcast.1, f32[128,16384]{1,0:T(8,128)} %all-gather.8.cloned.1.call-done, f32[128]{0:T(128)S(1)} %select_reduce_fusion, ...), kind=kOutput, calls=%fused_computation.79 | convolution fusion | flops 820518912 | bytes 16778380 | tf_op jit(solution)/shard_map/dot_general | solution.py:120
  335.7 5.9 %all-reduce.1 = (f32[32]{0:T(128)S(1)}, f32[32]{0:T(128)S(1)}, f32[32]{0:T(128)S(1)}) all-reduce(f32[32]{0:T(128)S(1)} %get-tuple-element.14, f32[32]{0:T(128)S(1)} %get-tuple-element.13, f32[32]{0:T(128)S(1)} %get-tuple-element.12), channel_id=1, replica_groups=mesh['tm'=8,'node'=4] {'node'}, use_global_device_ids=true, to_apply=%region_10.11 | all-reduce | flops 96 | bytes 768 | tf_op jit(solution)/shard_map/psum | solution.py:126
  341.6 21.8 %all-reduce = (f32[1,32]{1,0:T(1,128)S(1)}, f32[1,32]{1,0:T(1,128)S(1)}, f32[1,32]{1,0:T(1,128)S(1)}) all-reduce(f32[1,32]{1,0:T(1,128)S(1)} %bitcast.27, f32[1,32]{1,0:T(1,128)S(1)} %bitcast.28, f32[1,32]{1,0:T(1,128)S(1)} %bitcast.29), channel_id=1, replica_groups=mesh['tm'=8,'node'=4] {'tm'}, use_global_device_ids=true, to_apply=%region_11.12 | all-reduce | flops 96 | bytes 768 | tf_op jit(solution)/shard_map/psum | solution.py:126
  363.4 0.6 fusion.71
  (2 shorter events, 0.0 us)
Async XLA Ops:
  7.2 68.0 %all-gather.4.cloned.1.call-start = ((), (), s32[]{:S(2)}) async-start(), calls=%async_computation | async-start | bytes 10485760 | tf_op jit(solution)/shard_map/all_gather | solution.py:107
  8.0 3.1 copy-start
  8.0 3.5 copy-start.1
  14.0 6.4 %copy-start.5 = (f32[4]{0:T(128)S(1)}, f32[4]{0:T(128)}, u32[]{:S(2)}) copy-start(f32[4]{0:T(128)} %constant.74.clone) | copy-start | bytes 52
  14.0 126.2 %all-reduce.5.cloned.1.call-start = ((), (), s32[]{:S(2)}) async-start(), calls=%async_computation.1 | async-start | bytes 4194304 | tf_op jit(solution)/shard_map/psum | solution.py:15
  14.1 50.1 %collective-permute-start = (f32[32,16384]{1,0:T(8,128)}, f32[32,16384]{1,0:T(8,128)}, u32[]{:S(2)}, u32[]{:S(2)}) collective-permute-start(f32[32,16384]{1,0:T(8,128)} %bitcast.26), channel_id=1, source_target_pairs={{0,4},{4,8},{8,12},{12,16},{16,20},{20,24},{24,28},{1,5},{5,9},{9,... | collective-permute-start | bytes 6291464 | tf_op jit(solution)/shard_map/ppermute | solution.py:21
  85.6 2.7 copy-start.4
  88.4 111.8 %all-gather.6.cloned.1.call-start = ((), (), s32[]{:S(2)}) async-start(), calls=%async_computation.2 | async-start | bytes 10485760 | tf_op jit(solution)/shard_map/all_gather | solution.py:107
  93.8 171.7 %all-reduce.7.cloned.1.call-start = ((), (), s32[]{:S(2)}) async-start(), calls=%async_computation.3 | async-start | bytes 4194304 | tf_op jit(solution)/shard_map/psum | solution.py:15
  140.2 48.3 %collective-permute-start.1 = (f32[32,16384]{1,0:T(8,128)}, f32[32,16384]{1,0:T(8,128)}, u32[]{:S(2)}, u32[]{:S(2)}) collective-permute-start(f32[32,16384]{1,0:T(8,128)} %all-reduce.5.cloned.1.call-done), channel_id=1, source_target_pairs={{0,4},{4,8},{8,12},{12,16},{16,20},{20,24},{24,28},{1,5},{5,9},{9,... | collective-permute-start | bytes 6291464 | tf_op jit(solution)/shard_map/ppermute | solution.py:21
  210.9 2.7 copy-start.3
  213.7 111.6 %all-gather.8.cloned.1.call-start = ((), (), s32[]{:S(2)}) async-start(), calls=%async_computation.4 | async-start | bytes 10485760 | tf_op jit(solution)/shard_map/all_gather | solution.py:107
  219.2 106.1 %copy-start.2 = (f32[1,32,16384]{2,1,0:T(8,128)S(1)}, f32[1,32,16384]{2,1,0:T(8,128)}, u32[]{:S(2)}) copy-start(f32[1,32,16384]{2,1,0:T(8,128)} %param.4) | copy-start | bytes 6291460
  265.5 48.3 %collective-permute-start.2 = (f32[32,16384]{1,0:T(8,128)}, f32[32,16384]{1,0:T(8,128)}, u32[]{:S(2)}, u32[]{:S(2)}) collective-permute-start(f32[32,16384]{1,0:T(8,128)} %all-reduce.7.cloned.1.call-done), channel_id=1, source_target_pairs={{0,4},{4,8},{8,12},{12,16},{16,20},{20,24},{24,28},{1,5},{5,9},{9,... | collective-permute-start | bytes 6291464 | tf_op jit(solution)/shard_map/ppermute | solution.py:21
Sparse Core Ops, SparseCore 0:
  14.1 60.9 all-gather.3
  88.5 51.6 all-reduce.4
  141.8 58.3 all-gather.5
  213.8 51.6 all-reduce.6
  266.9 58.3 all-gather.7
